TPU v7x, 32 devices: a whole 2x2x4 slice. The times are simulated.
32 devices in a mesh: ep: 4 (over y, x), dp: 2 (over core), tp: 4 (over z).
Axes of the slice: x: 2, y: 2, z: 4, core: 2. Of those that a mesh axis runs over, the one named last changes fastest.
Arguments:
- tokens: bfloat16 [192, 7168], P(('ep', 'dp')), may hold values from -6 to 6
- expert_ids: int32 [192, 8], P(('ep', 'dp')), may hold values from 0 to 31, all different within a row; in each aligned block of 24 rows (0 to 23, 24 to 47, ...) at most 8 rows name the same one
- route_weight: float32 [192, 8], P(('ep', 'dp')), may hold values from 0.1 to 0.6
- gate_weight: bfloat16 [32, 7168, 1536], P('ep', None, 'tp'), may hold values from -0.0625 to 0.0625
- up_weight: bfloat16 [32, 7168, 1536], P('ep', None, 'tp'), may hold values from -0.0625 to 0.0625
- down_weight: bfloat16 [32, 1536, 7168], P('ep', 'tp'), may hold values from -0.15625 to 0.15625
Outputs:
- moe_out: bfloat16 [192, 7168], P(('ep', 'dp', 'tp'))
Inputs may be any that keep to these rules, and one draw needn't show every extreme that they name: `expert_ids`: each row names 8 different experts. In every aligned block of 24 rows no expert is named by more than 8 rows, a bound that some block reaches.
All inputs are finite; a program needn't handle non-finite values.
Results may differ from a plain program's by a relative error of at most 0.0049.
Values may be sent and summed in bfloat16 or wider, within the bound.
A program may use at most 192 MiB of HBM per device.

v0:
```python
from functools import partial

import jax
import jax.numpy as jnp
from jax import lax
from jax.experimental import pallas as pl
from jax.experimental.pallas import tpu as pltpu
from jax.sharding import PartitionSpec as P

TOP = 8
EXPERTS = 32
MOST = 8
MESH = pl.DeviceIdType.MESH
VMEM_BYTES = 67_000_000


def expert_block(received, gate_weight, up_weight, down_weight):
    ep_size = lax.axis_size("ep")
    local_count = gate_weight.shape[0]
    slot_count = received.shape[1]
    width = received.shape[2]
    shaped = received.reshape(ep_size, local_count, slot_count, width)
    gate_proj = jnp.einsum(
        "sxmd,xdf->sxmf", shaped, gate_weight, preferred_element_type=jnp.float32
    )
    up_proj = jnp.einsum("sxmd,xdf->sxmf", shaped, up_weight, preferred_element_type=jnp.float32)
    hidden = (jax.nn.silu(gate_proj) * up_proj).astype(jnp.bfloat16)
    partial_rows = jnp.einsum(
        "sxmf,xfd->sxmd", hidden, down_weight, preferred_element_type=jnp.float32
    )
    partial_rows = partial_rows.reshape(ep_size * local_count, slot_count, width)
    return lax.all_to_all(partial_rows, "ep", split_axis=0, concat_axis=0, tiled=True)


def build_rows(source, per_token):
    width = source.shape[1]
    dispatch = jnp.any(per_token, 1).astype(jnp.bfloat16)
    outgoing = jnp.einsum("tp,td->pd", dispatch, source, preferred_element_type=jnp.float32).astype(
        jnp.bfloat16
    )
    return outgoing.reshape(EXPERTS, MOST, width)


def combine_rows(returned, per_token, route_weight):
    weight_table = jnp.sum(per_token.astype(jnp.float32) * route_weight[:, :, None], 1)
    combined = jnp.dot(weight_table, returned, precision=lax.Precision.HIGHEST)
    return combined


def per_device(tokens, expert_ids, route_weight, gate_weight, up_weight, down_weight):
    rows_here = tokens.shape[0]
    width = tokens.shape[1]
    capacity = EXPERTS * MOST
    chosen = expert_ids.reshape(-1)
    onehot = (chosen[:, None] == jnp.arange(EXPERTS, dtype=jnp.int32)[None, :]).astype(jnp.int32)
    earlier = jnp.cumsum(onehot, 0) - onehot
    slot_index = jnp.sum(earlier * onehot, 1)
    position = chosen * MOST + slot_index
    matches = position[:, None] == jnp.arange(capacity, dtype=jnp.int32)[None, :]
    per_token = matches.reshape(rows_here, TOP, capacity)
    outgoing = build_rows(tokens, per_token)
    worker = partial(
        expert_block, gate_weight=gate_weight, up_weight=up_weight, down_weight=down_weight
    )
    returned = worker(lax.all_to_all(outgoing, "ep", split_axis=0, concat_axis=0, tiled=True))
    returned = returned.reshape(capacity, width)
    combined = combine_rows(returned, per_token, route_weight)
    summed = lax.psum_scatter(combined, "tp", scatter_dimension=0, tiled=True)
    return summed.astype(jnp.bfloat16)


def xor_bit(index, bit):
    return index + bit - 2 * bit * ((index // bit) % 2)


def xor_any(index, mask):
    bit = 1
    while bit <= mask:
        if mask & bit:
            index = xor_bit(index, bit)
        bit *= 2
    return index


def rotated(bits, turn):
    turn %= len(bits)
    return bits[turn:] + bits[:turn]


def moe_kernel(
    n_ep, n_tp, chunks, ring,
    tok_ref, ids_ref, rw_ref, gate_ref, up_ref, down_ref,
    out_ref,
    xs, ids_all, rw_all, gu, dn, acc, hid, own, pair_out, pair_in, half_out, half_in,
    last_keep, last_out, last_in,
    in_sem, small_send, small_recv, ag_send, ag_recv, gu_sem, dn_sem,
    pair_send, pair_recv, half_send, half_recv, last_send, last_recv,
):
    ep, dp, tp = lax.axis_index("ep"), lax.axis_index("dp"), lax.axis_index("tp")
    rows = tok_ref.shape[0]
    depth = xs.shape[2]
    units = gate_ref.shape[2]
    experts = hid.shape[1] // units
    blocks = dn.shape[0]
    wide = dn.shape[3]
    half_rows = n_ep * rows
    out_rows = rows // n_tp
    bits = [1 << i for i in range(n_ep.bit_length() - 1)]
    first_expert = dp * experts
    sibling = {"dp": 1 - dp}

    def gu_copies(item):
        chunk, expert = item // experts, item % experts
        slot = item % ring
        src_rows = pl.ds(chunk * depth, depth)
        return [
            pltpu.make_async_copy(
                ref.at[first_expert + expert, src_rows, :],
                gu.at[slot, :, pl.ds(at * units, units)],
                gu_sem.at[slot, at],
            )
            for at, ref in enumerate((gate_ref, up_ref))
        ]

    def dn_copy(n):
        return pltpu.make_async_copy(
            down_ref.at[pl.ds(first_expert, experts), :, pl.ds(n * wide, wide)],
            dn.at[n],
            dn_sem.at[n],
        )

    inputs = [
        pltpu.make_async_copy(
            tok_ref.at[:, pl.ds(k * depth, depth)], xs.at[k, pl.ds(0, rows), :], in_sem.at[k]
        )
        for k in range(chunks)
    ]
    inputs.append(pltpu.make_async_copy(ids_ref, ids_all.at[pl.ds(0, rows), :], in_sem.at[chunks]))
    inputs.append(pltpu.make_async_copy(rw_ref, rw_all.at[pl.ds(0, rows), :], in_sem.at[chunks + 1]))
    for copy in inputs:
        copy.start()
    items = chunks * experts
    for item in range(min(ring, items)):
        for copy in gu_copies(item):
            copy.start()
    for n in range(blocks):
        dn_copy(n).start()

    group = [(q, other) for other in range(2) for q in range(n_ep) if (q, other) != (0, 0)]
    barrier = pltpu.get_barrier_semaphore()
    for q, other in group:
        pl.semaphore_signal(
            barrier, inc=1, device_id={"ep": xor_any(ep, q), "dp": 1 - dp if other else dp},
            device_id_type=MESH,
        )
    for step in range(1, n_tp):
        pl.semaphore_signal(
            barrier, inc=1, device_id={"tp": lax.rem(tp + step, n_tp)}, device_id_type=MESH
        )
    pl.semaphore_wait(barrier, len(group) + n_tp - 1)
    for copy in inputs:
        copy.wait()

    def remote(src, dst, send, recv, device):
        return pltpu.make_async_remote_copy(
            src_ref=src, dst_ref=dst, send_sem=send, recv_sem=recv, device_id=device,
            device_id_type=MESH,
        )

    def gather_step(k, step):
        have = [0]
        order = rotated(bits, k)
        for bit in order[:step]:
            have = have + [q ^ bit for q in have]
        bit = order[step]
        return [
            remote(
                xs.at[k, pl.ds(q * rows, rows), :],
                xs.at[k, pl.ds((q ^ bit) * rows, rows), :],
                ag_send.at[k, q ^ bit],
                ag_recv.at[k, q ^ bit],
                {"ep": xor_bit(ep, bit)},
            )
            for q in have
        ]

    def gather_pair(k):
        return remote(
            xs.at[k, pl.ds(0, half_rows), :],
            xs.at[k, pl.ds(half_rows, half_rows), :],
            ag_send.at[k, 0],
            ag_recv.at[k, 0],
            sibling,
        )

    sent = []

    def send(copy):
        copy.start()
        sent.append(copy)

    for k in range(chunks):
        for copy in gather_step(k, 0):
            send(copy)
    small = []
    for at, (q, other) in enumerate(group):
        device = {"ep": xor_any(ep, q), "dp": 1 - dp if other else dp}
        row = (other * n_ep + q) * rows
        for kind, ref in enumerate((ids_all, rw_all)):
            small.append(
                remote(
                    ref.at[pl.ds(0, rows), :], ref.at[pl.ds(row, rows), :],
                    small_send.at[at, kind], small_recv.at[at, kind], device,
                )
            )
    for copy in small:
        send(copy)
    for step in range(1, len(bits)):
        for k in range(chunks):
            for copy in gather_step(k, step - 1):
                copy.wait_recv()
            for copy in gather_step(k, step):
                send(copy)

    def finish_gather(k):
        for copy in gather_step(k, len(bits) - 1):
            copy.wait_recv()
        send(gather_pair(k))

    finish_gather(0)
    for k in range(chunks):
        if k + 1 < chunks:
            finish_gather(k + 1)
        gather_pair(k).wait_recv()

        def product(j, carry, k=k):
            item = k * experts + j
            slot = item % ring
            for copy in gu_copies(item):
                copy.wait()
            value = jnp.dot(xs[k], gu[slot], preferred_element_type=jnp.float32)
            if k == 0:
                acc[j] = value
            else:
                acc[j] += value

            @pl.when(item + ring < items)
            def _():
                for copy in gu_copies(item + ring):
                    copy.start()

            return carry

        lax.fori_loop(0, experts, product, 0)

    for copy in small:
        copy.wait_recv()
    base = ep * (2 * experts) + first_expert
    for j in range(experts):
        weight = jnp.sum(jnp.where(ids_all[...] == base + j, rw_all[...], 0.0), 1, keepdims=True)
        gate, up = acc[j, :, :units], acc[j, :, units:]
        hidden = gate / (1.0 + jnp.exp(-gate)) * up * weight
        hid[:, j * units : (j + 1) * units] = hidden.astype(jnp.bfloat16)

    def pair_copy(n):
        return remote(pair_out.at[n], pair_in.at[n], pair_send.at[n], pair_recv.at[n], sibling)

    def split(n, step):
        kept = list(range(n_ep))
        order = rotated(bits, n)
        for bit in order[:step]:
            kept = [q for q in kept if not q & bit]
        bit = order[step]
        return bit, [q for q in kept if not q & bit], [q for q in kept if q & bit]

    offsets = [sum(n_ep >> (s + 1) for s in range(step)) for step in range(len(bits))]

    def half_copy(n, step):
        bit, _, away = split(n, step)
        part = pl.ds(offsets[step], len(away))
        return remote(
            half_out.at[n, part], half_in.at[n, part], half_send.at[n, step],
            half_recv.at[n, step], {"ep": xor_bit(ep, bit)},
        )

    def last_copy(n, step):
        peer = lax.rem(tp + step, n_tp)
        return remote(
            last_out.at[n, peer], last_in.at[n, step - 1], last_send.at[n, step - 1],
            last_recv.at[n, step - 1], {"tp": peer},
        )

    def arrived(n, step):
        if step == 0:
            pair_copy(n).wait_recv()
            return lambda q: own[n, q] + pair_in[n, q]
        half_copy(n, step - 1).wait_recv()
        _, kept, _ = split(n, step - 1)
        start = offsets[step - 1]
        return lambda q: own[n, q] + half_in[n, start + kept.index(q)].astype(jnp.float32)

    def reduce_step(n, step):
        total = arrived(n, step)
        if step < len(bits):
            _, kept, away = split(n, step)
            for i, q in enumerate(away):
                half_out[n, offsets[step] + i] = total(q).astype(jnp.bfloat16)
            send(half_copy(n, step))
            for q in kept:
                own[n, q] = total(q)
        else:
            value = total(0)
            for t in range(n_tp):
                piece = value[t * out_rows : (t + 1) * out_rows]
                last_keep[n, t] = piece
                last_out[n, t] = piece.astype(jnp.bfloat16)
            for t in range(1, n_tp):
                send(last_copy(n, t))

    def finish(n):
        value = last_keep[n, tp]
        for t in range(1, n_tp):
            last_copy(n, t).wait_recv()
            value += last_in[n, t - 1].astype(jnp.float32)
        out_ref[:, n * wide : (n + 1) * wide] = value.astype(out_ref.dtype)

    for n in range(blocks):
        dn_copy(n).wait()
        value = jnp.dot(
            hid[...], dn[n].reshape(experts * units, wide), preferred_element_type=jnp.float32
        )
        for q in range(n_ep):
            pair_out[n, q] = value[half_rows + q * rows : half_rows + (q + 1) * rows]
            own[n, q] = value[q * rows : (q + 1) * rows]
        send(pair_copy(n))
        if n > 0:
            reduce_step(n - 1, 0)
    reduce_step(blocks - 1, 0)
    lag = 2
    stages = len(bits) + 1
    for turn in range(blocks + lag * (stages - 1)):
        for stage in range(stages):
            n = turn - lag * stage
            if 0 <= n < blocks:
                if stage < len(bits):
                    reduce_step(n, stage + 1)
                else:
                    finish(n)
    for copy in sent:
        copy.wait_send()


def fused_plan(mesh, rows, width, local_count, units):
    n_ep, n_dp, n_tp = (mesh.shape[a] for a in ("ep", "dp", "tp"))
    if n_dp != 2 or local_count % 2 or n_ep < 2 or n_ep & (n_ep - 1) or rows % 8 or rows % n_tp:
        return None
    experts = local_count // 2
    if units % 128 or width % 256:
        return None
    groups = width // 256
    chunks = next((c for c in (4, 2, 1) if groups % c == 0))
    tiles = max(t for t in range(1, 5) if groups % t == 0)
    wide = 256 * tiles
    depth = width // chunks
    total_rows = 2 * n_ep * rows
    held = total_rows * width * 2 + experts * total_rows * units * 10 + 2 * experts * units * width
    held += 3 * n_ep * rows * width * 4 + 4 * (n_ep - 1) * -(-rows // 16) * 16 * width
    held += n_tp * width * 96 + total_rows * wide * 4 + 2_000_000
    slot = depth * 2 * units * 2
    ring = min(chunks * experts, (VMEM_BYTES - held) // slot)
    if ring < 2:
        return None
    return chunks, wide, ring


def fused(mesh, plan, tokens, expert_ids, route_weight, gate_weight, up_weight, down_weight):
    chunks, wide, ring = plan
    n_ep, n_tp = mesh.shape["ep"], mesh.shape["tp"]
    rows, width = tokens.shape
    units = gate_weight.shape[2]
    experts = gate_weight.shape[0] // 2
    depth, blocks = width // chunks, width // wide
    total_rows = 2 * n_ep * rows
    out_rows = rows // n_tp
    steps = n_ep.bit_length() - 1
    top = expert_ids.shape[1]
    peers = 2 * n_ep - 1
    dma = pltpu.SemaphoreType.DMA
    f32, bf16 = jnp.float32, jnp.bfloat16
    return pl.pallas_call(
        partial(moe_kernel, n_ep, n_tp, chunks, ring),
        out_shape=jax.ShapeDtypeStruct((out_rows, width), bf16),
        in_specs=[pl.BlockSpec(memory_space=pltpu.HBM)] * 6,
        out_specs=pl.BlockSpec(memory_space=pltpu.VMEM),
        scratch_shapes=[
            pltpu.VMEM((chunks, total_rows, depth), bf16),
            pltpu.VMEM((total_rows, top), jnp.int32),
            pltpu.VMEM((total_rows, top), f32),
            pltpu.VMEM((ring, depth, 2 * units), bf16),
            pltpu.VMEM((blocks, experts, units, wide), bf16),
            pltpu.VMEM((experts, total_rows, 2 * units), f32),
            pltpu.VMEM((total_rows, experts * units), bf16),
            pltpu.VMEM((blocks, n_ep, rows, wide), f32),
            pltpu.VMEM((blocks, n_ep, rows, wide), f32),
            pltpu.VMEM((blocks, n_ep, rows, wide), f32),
            pltpu.VMEM((blocks, n_ep - 1, rows, wide), bf16),
            pltpu.VMEM((blocks, n_ep - 1, rows, wide), bf16),
            pltpu.VMEM((blocks, n_tp, out_rows, wide), f32),
            pltpu.VMEM((blocks, n_tp, out_rows, wide), bf16),
            pltpu.VMEM((blocks, n_tp - 1, out_rows, wide), bf16),
            dma((chunks + 2,)),
            dma((peers, 2)),
            dma((peers, 2)),
            dma((chunks, n_ep)),
            dma((chunks, n_ep)),
            dma((ring, 2)),
            dma((blocks,)),
            dma((blocks,)),
            dma((blocks,)),
            dma((blocks, steps)),
            dma((blocks, steps)),
            dma((blocks, n_tp - 1)),
            dma((blocks, n_tp - 1)),
        ],
        compiler_params=pltpu.CompilerParams(
            collective_id=0, has_side_effects=True, vmem_limit_bytes=VMEM_BYTES
        ),
    )(tokens, expert_ids, route_weight, gate_weight, up_weight, down_weight)


def solution(mesh):
    in_specs = (
        P(("ep", "dp"), None),
        P(("ep", "dp"), None),
        P(("ep", "dp"), None),
        P("ep", None, "tp"),
        P("ep", None, "tp"),
        P("ep", "tp", None),
    )
    out_specs = P(("ep", "dp", "tp"), None)

    def body(*arrays):
        rows, width = arrays[0].shape
        local_count, _, units = arrays[3].shape
        plan = fused_plan(mesh, rows, width, local_count, units)
        if plan is None:
            return per_device(*arrays)
        return fused(mesh, plan, *arrays)

    return jax.shard_map(body, mesh=mesh, in_specs=in_specs, out_specs=out_specs, check_vma=False)
```

profile of v0, /device:TPU:0, one launch (start us, length us, event | category | flops | bytes accessed | tf_op | source)
XLA Modules:
  0.0 72.7 jit_solution(6245240986884290702)
XLA Ops:
  0.0 1.4 %copy.7.ids_ref = s32[24,8]{1,0:T(8,128)} copy(s32[24,8]{0,1:T(8,128)} %param.7) | data formatting | bytes 1536 | tf_op args[1]
  1.4 1.4 %copy.8.rw_ref = f32[24,8]{1,0:T(8,128)} copy(f32[24,8]{0,1:T(8,128)} %param.8) | data formatting | bytes 1536 | tf_op args[2]
  2.7 68.4 %shard_map.64 = bf16[6,7168]{1,0:T(8,128)(2,1)} custom-call(bf16[24,7168]{1,0:T(8,128)(2,1)} %tok_ref.1, s32[24,8]{1,0:T(8,128)} %copy.7.ids_ref, f32[24,8]{1,0:T(8,128)} %copy.8.rw_ref, bf16[8,7168,384]{2,1,0:T(8,128)(2,1)} %gate_ref.1, bf16[8,7168,384]{2,1,0:T(8,128)(2,1)} %up_ref.1, bf16[8,384,7168]{2,1,0:T(8,128)(2,1)} %down_ref.1), custom_call_target="tpu_custom_call" | custom-call | tf_op jit(solution)/shard_map/pallas_call | solution.py:390
  71.1 1.6 %copy.10 = bf16[6,7168]{1,0:T(8,128)(2,1)} copy(bf16[6,7168]{1,0:T(8,128)(2,1)} %shard_map.64) | data formatting | bytes 172032
where the time goes:
time: 72.9 us; the launch traced here: 72.7 us
  Pallas kernels  68.4 us (94%)
  local copies, waits for them, and re-layouts  4.27 us (6%)
    pallas_call x1, Pallas kernels, fused(): pl.pallas_call(partial(moe_kernel, n_ep, n_tp, chunks, ring), out_shape=j...  68.4 us
    unnamed x3, local copies, waits for them, and re-layouts  4.27 us

commit v1 on v0

v1 whole, which is shorter than its diff:
```python
from functools import partial

import jax
import jax.numpy as jnp
from jax import lax
from jax.experimental import pallas as pl
from jax.experimental.pallas import tpu as pltpu
from jax.sharding import PartitionSpec as P

TOP = 8
EXPERTS = 32
MOST = 8
MESH = pl.DeviceIdType.MESH
VMEM_BYTES = 67_000_000
AHEAD = 4
EARLY = 5
LAGS = (3, 5, 9)


def expert_block(received, gate_weight, up_weight, down_weight):
    ep_size = lax.axis_size("ep")
    local_count = gate_weight.shape[0]
    slot_count = received.shape[1]
    width = received.shape[2]
    shaped = received.reshape(ep_size, local_count, slot_count, width)
    gate_proj = jnp.einsum(
        "sxmd,xdf->sxmf", shaped, gate_weight, preferred_element_type=jnp.float32
    )
    up_proj = jnp.einsum("sxmd,xdf->sxmf", shaped, up_weight, preferred_element_type=jnp.float32)
    hidden = (jax.nn.silu(gate_proj) * up_proj).astype(jnp.bfloat16)
    partial_rows = jnp.einsum(
        "sxmf,xfd->sxmd", hidden, down_weight, preferred_element_type=jnp.float32
    )
    partial_rows = partial_rows.reshape(ep_size * local_count, slot_count, width)
    return lax.all_to_all(partial_rows, "ep", split_axis=0, concat_axis=0, tiled=True)


def build_rows(source, per_token):
    width = source.shape[1]
    dispatch = jnp.any(per_token, 1).astype(jnp.bfloat16)
    outgoing = jnp.einsum("tp,td->pd", dispatch, source, preferred_element_type=jnp.float32).astype(
        jnp.bfloat16
    )
    return outgoing.reshape(EXPERTS, MOST, width)


def combine_rows(returned, per_token, route_weight):
    weight_table = jnp.sum(per_token.astype(jnp.float32) * route_weight[:, :, None], 1)
    combined = jnp.dot(weight_table, returned, precision=lax.Precision.HIGHEST)
    return combined


def per_device(tokens, expert_ids, route_weight, gate_weight, up_weight, down_weight):
    rows_here = tokens.shape[0]
    width = tokens.shape[1]
    capacity = EXPERTS * MOST
    chosen = expert_ids.reshape(-1)
    onehot = (chosen[:, None] == jnp.arange(EXPERTS, dtype=jnp.int32)[None, :]).astype(jnp.int32)
    earlier = jnp.cumsum(onehot, 0) - onehot
    slot_index = jnp.sum(earlier * onehot, 1)
    position = chosen * MOST + slot_index
    matches = position[:, None] == jnp.arange(capacity, dtype=jnp.int32)[None, :]
    per_token = matches.reshape(rows_here, TOP, capacity)
    outgoing = build_rows(tokens, per_token)
    worker = partial(
        expert_block, gate_weight=gate_weight, up_weight=up_weight, down_weight=down_weight
    )
    returned = worker(lax.all_to_all(outgoing, "ep", split_axis=0, concat_axis=0, tiled=True))
    returned = returned.reshape(capacity, width)
    combined = combine_rows(returned, per_token, route_weight)
    summed = lax.psum_scatter(combined, "tp", scatter_dimension=0, tiled=True)
    return summed.astype(jnp.bfloat16)


def xor_bit(index, bit):
    return index + bit - 2 * bit * ((index // bit) % 2)


def xor_any(index, mask):
    bit = 1
    while bit <= mask:
        if mask & bit:
            index = xor_bit(index, bit)
        bit *= 2
    return index


def rotated(bits, turn):
    turn %= len(bits)
    return bits[turn:] + bits[:turn]


def moe_kernel(
    n_ep, n_tp, ring, early,
    tok_ref, ids_ref, rw_ref, gate_ref, up_ref, down_ref,
    out_ref,
    xs, ids_own, rw_own, ids_all, rw_all, gu, dn, acc, hid, own, out0, in0, out1, in1,
    last_keep, last_out, last_in,
    in_sem, small_send, small_recv, ag_send, ag_recv, gu_sem, dn_sem, hid_send, hid_recv,
    fold_send, fold_recv, last_send, last_recv,
):
    ep, dp, tp = lax.axis_index("ep"), lax.axis_index("dp"), lax.axis_index("tp")
    rows = tok_ref.shape[0]
    chunks, sides, groups, _, step_width = xs.shape
    units = gate_ref.shape[2]
    pairs = acc.shape[0]
    depth = gu.shape[1]
    items = chunks * pairs
    experts = 2 * pairs
    blocks = dn.shape[0]
    wide = dn.shape[3]
    half = blocks * wide
    sub = wide // 2
    total_rows = groups * rows
    half_rows = n_ep * rows
    out_rows = rows // n_tp
    bits = [1 << i for i in range(n_ep.bit_length() - 1)]
    first_expert = dp * experts
    other_first = (1 - dp) * experts
    sibling = {"dp": 1 - dp}
    column = dp * half

    def arrived(ref, sem):
        pltpu.make_async_copy(ref, ref, sem).wait()

    def start_gu(item):
        chunk, pair = item // pairs, item % pairs
        slot = item % ring
        for e in range(2):
            for at, ref in enumerate((gate_ref, up_ref)):
                pltpu.make_async_copy(
                    ref.at[first_expert + 2 * pair + e, pl.ds(chunk * depth, depth), :],
                    gu.at[slot, :, pl.ds((2 * e + at) * units, units)],
                    gu_sem.at[slot],
                ).start()

    def start_dn(n):
        cols = pl.ds(pl.multiple_of(column + n * wide, 128), wide)
        for at, first in enumerate((first_expert, other_first)):
            pltpu.make_async_copy(
                down_ref.at[pl.ds(first, experts), :, cols],
                dn.at[n, pl.ds(at * experts, experts)],
                dn_sem.at[n],
            ).start()

    for chunk in range(chunks):
        for side in range(sides):
            pltpu.make_async_copy(
                tok_ref.at[:, pl.ds((chunk * sides + side) * step_width, step_width)],
                xs.at[chunk, side, 0],
                in_sem.at[0],
            ).start()
    small_in = [
        pltpu.make_async_copy(ids_ref, ids_own, in_sem.at[1]),
        pltpu.make_async_copy(rw_ref, rw_own, in_sem.at[2]),
    ]
    for copy in small_in:
        copy.start()

    group = [(q, other) for other in range(2) for q in range(n_ep) if (q, other) != (0, 0)]
    barrier = pltpu.get_barrier_semaphore()
    for q, other in group:
        pl.semaphore_signal(
            barrier, inc=1, device_id={"ep": xor_any(ep, q), "dp": 1 - dp if other else dp},
            device_id_type=MESH,
        )
    for step in range(1, n_tp):
        for to in (dp, 1 - dp):
            pl.semaphore_signal(
                barrier, inc=1, device_id={"dp": to, "tp": lax.rem(tp + step, n_tp)},
                device_id_type=MESH,
            )
    with jax.named_scope("inwait"):
        arrived(xs.at[:, :, 0], in_sem.at[0])
        for copy in small_in:
            copy.wait()
    for item in range(min(early, items)):
        start_gu(item)
    ids_all[:rows, :] = ids_own[...].T
    rw_all[:rows, :] = rw_own[...].T
    with jax.named_scope("barrier"):
        pl.semaphore_wait(barrier, len(group) + 2 * (n_tp - 1))

    def send(src, dst, send_sem, recv_sem, device):
        pltpu.make_async_remote_copy(
            src_ref=src, dst_ref=dst, send_sem=send_sem, recv_sem=recv_sem, device_id=device,
            device_id_type=MESH,
        ).start()

    def gather(chunk, step):
        for side in range(sides):
            order = rotated(bits, side)
            have = [0]
            for bit in order[:step]:
                have = have + [q ^ bit for q in have]
            bit = order[step]
            for q in have:
                send(
                    xs.at[chunk, side, q], xs.at[chunk, side, q ^ bit],
                    ag_send, ag_recv.at[chunk, step], {"ep": xor_bit(ep, bit)},
                )

    def gathered(chunk, step):
        with jax.named_scope(f"ag{step}#k={chunk}"):
            arrived(xs.at[chunk, :, pl.ds(0, 1 << step)], ag_recv.at[chunk, step])

    def gather_pair(chunk):
        gathered(chunk, 1)
        send(
            xs.at[chunk, :, pl.ds(0, n_ep)], xs.at[chunk, :, pl.ds(n_ep, n_ep)],
            ag_send, ag_recv.at[chunk, 2], sibling,
        )

    lead = min(AHEAD, chunks)
    for chunk in range(lead):
        gather(chunk, 0)
    for q, other in group:
        device = {"ep": xor_any(ep, q), "dp": 1 - dp if other else dp}
        row = (other * n_ep + q) * rows
        for kind, ref in enumerate((ids_all, rw_all)):
            send(
                ref.at[pl.ds(0, rows), :], ref.at[pl.ds(row, rows), :],
                small_send.at[kind], small_recv.at[kind], device,
            )
    asked = 0

    def relay():
        nonlocal asked
        if asked < chunks:
            gathered(asked, 0)
            gather(asked, 1)
            if asked + lead < chunks:
                gather(asked + lead, 0)
            asked += 1

    for _ in range(lead):
        relay()
    for item in range(early, min(ring, items)):
        start_gu(item)

    def product(chunk, pair):
        slot = (chunk * pairs + pair) % ring
        value = 0.0
        for side in range(sides):
            value += jnp.dot(
                xs[chunk, side].reshape(total_rows, step_width),
                gu[slot, side * step_width : (side + 1) * step_width],
                preferred_element_type=jnp.float32,
            )
        return value

    base = ep * (2 * experts) + first_expert
    started = 0
    gather_pair(0)
    for chunk in range(chunks):
        relay()
        if chunk + 1 < chunks:
            gather_pair(chunk + 1)
        with jax.named_scope(f"pairwait#k={chunk}"):
            arrived(xs.at[chunk, :, pl.ds(n_ep, n_ep)], ag_recv.at[chunk, 2])
        if chunk + 1 < chunks:
            with jax.named_scope(f"guwait#k={chunk}"):
                for pair in range(pairs):
                    slot = (chunk * pairs + pair) % ring
                    arrived(gu.at[slot], gu_sem.at[slot])
            with jax.named_scope(f"gateup#k={chunk}"):
                for pair in range(pairs):
                    value = product(chunk, pair)
                    if chunk == 0:
                        acc[pair] = value
                    else:
                        acc[pair] += value
            for pair in range(pairs):
                item = chunk * pairs + pair + ring
                if item < items:
                    start_gu(item)
            while started < blocks and started < (chunk + 1) * pairs - (items - ring) + 2:
                start_dn(started)
                started += 1
    while started < blocks:
        start_dn(started)
        started += 1

    for kind, ref in enumerate((ids_all, rw_all)):
        arrived(ref.at[pl.ds(rows, total_rows - rows)], small_recv.at[kind])
    for pair in range(pairs):
        with jax.named_scope(f"last#p={pair}"):
            slot = ((chunks - 1) * pairs + pair) % ring
            arrived(gu.at[slot], gu_sem.at[slot])
            value = product(chunks - 1, pair)
            if chunks > 1:
                value += acc[pair]
            for e in range(2):
                weight = jnp.sum(
                    jnp.where(ids_all[...] == base + 2 * pair + e, rw_all[...], 0.0), 1, keepdims=True
                )
                gate = value[:, 2 * e * units : (2 * e + 1) * units]
                up = value[:, (2 * e + 1) * units : (2 * e + 2) * units]
                hidden = gate / (1.0 + jnp.exp(-gate)) * up * weight
                hid[pair, :, e * units : (e + 1) * units] = hidden.astype(jnp.bfloat16)
        for at in range(2):
            send(
                hid.at[pair, pl.ds(at * half_rows, half_rows), :],
                hid.at[pairs + pair, pl.ds((1 - at) * half_rows, half_rows), :],
                hid_send, hid_recv.at[pair], sibling,
            )

    def split(side, step):
        kept = list(range(n_ep))
        order = rotated(bits, side)
        for bit in order[:step]:
            kept = [q for q in kept if not q & bit]
        bit = order[step]
        return bit, [q for q in kept if not q & bit], [q for q in kept if q & bit]

    def fold_send_to(n, side, step):
        bit, _, _ = split(side, step)
        src, dst = ((out0, in0), (out1, in1))[step]
        send(
            src.at[n, side], dst.at[n, side], fold_send.at[step], fold_recv.at[n, step],
            {"ep": xor_bit(ep, bit)},
        )

    def down(n, low, high):
        value = 0.0
        for p in range(low, high):
            value += jnp.dot(
                hid[p], dn[n, 2 * p : 2 * p + 2].reshape(2 * units, wide),
                preferred_element_type=jnp.float32,
            )
        return value

    def store0(n, value):
        for side in range(2):
            _, kept, away = split(side, 0)
            cols = slice(side * sub, (side + 1) * sub)
            for d in range(2):
                for i, q in enumerate(away):
                    row = d * half_rows + q * rows
                    out0[n, side, d, i] = value[row : row + rows, cols].astype(jnp.bfloat16)
                for i, q in enumerate(kept):
                    row = d * half_rows + q * rows
                    own[n, side, d, i] = value[row : row + rows, cols]

    def fold0(n):
        for side in range(2):
            fold_send_to(n, side, 0)

    def fold1(n):
        arrived(in0.at[n], fold_recv.at[n, 0])
        for side in range(2):
            _, held, _ = split(side, 0)
            _, kept, away = split(side, 1)
            at_away, at_kept = held.index(away[0]), held.index(kept[0])
            for d in range(2):
                total = own[n, side, d, at_away] + in0[n, side, d, at_away].astype(jnp.float32)
                out1[n, side, d] = total.astype(jnp.bfloat16)
                own[n, side, d, at_kept] += in0[n, side, d, at_kept].astype(jnp.float32)
        for side in range(2):
            fold_send_to(n, side, 1)

    def fold2(n):
        arrived(in1.at[n], fold_recv.at[n, 1])
        for side in range(2):
            _, held, _ = split(side, 0)
            at_kept = held.index(0)
            cols = slice(side * sub, (side + 1) * sub)
            for d in range(2):
                total = own[n, side, d, at_kept] + in1[n, side, d].astype(jnp.float32)
                for t in range(n_tp):
                    piece = total[t * out_rows : (t + 1) * out_rows]
                    if d == 0:
                        last_keep[n, t, :, cols] = piece
                    last_out[n, d, t, :, cols] = piece.astype(jnp.bfloat16)
        for step in range(n_tp):
            peer = lax.rem(tp + step, n_tp)
            for other, to in enumerate((dp, 1 - dp)):
                if step or other:
                    send(
                        last_out.at[n, other, peer], last_in.at[n, step * 2 + other - 1],
                        last_send, last_recv.at[n], {"dp": to, "tp": peer},
                    )

    def finish(n):
        arrived(last_in.at[n], last_recv.at[n])
        for other in range(2):
            value = 0.0 if other else last_keep[n, tp]
            for step in range(n_tp):
                if step or other:
                    value += last_in[n, step * 2 + other - 1].astype(jnp.float32)
            start = (1 - dp if other else dp) * half + n * wide
            out_ref[:, pl.ds(pl.multiple_of(start, 128), wide)] = value.astype(out_ref.dtype)

    def stage(n, fn, name):
        if 0 <= n < blocks:
            with jax.named_scope(f"{name}#n={n}"):
                fn(n)

    first = min(2, blocks, pairs)
    for n in range(first):
        with jax.named_scope(f"down_own#n={n}"):
            arrived(dn.at[n], dn_sem.at[n])
            acc[n, :, :wide] = down(n, 0, pairs)
    with jax.named_scope("hidwait"):
        for pair in range(pairs):
            arrived(hid.at[pairs + pair], hid_recv.at[pair])
    for turn in range(blocks + LAGS[2]):
        if turn < blocks:
            with jax.named_scope(f"down#n={turn}"):
                if turn < first:
                    value = down(turn, pairs, 2 * pairs) + acc[turn, :, :wide]
                else:
                    arrived(dn.at[turn], dn_sem.at[turn])
                    value = down(turn, 0, 2 * pairs)
                store0(turn, value)
        stage(turn - LAGS[0], fold1, "fold1")
        stage(turn, fold0, "fold0")
        stage(turn - LAGS[1], fold2, "fold2")
        stage(turn - LAGS[2], finish, "finish")
    with jax.named_scope("tailsend"):
        arrived(xs.at[:, :, pl.ds(0, groups - 1)], ag_send)
        for kind, ref in enumerate((ids_all, rw_all)):
            arrived(ref.at[pl.ds(rows, total_rows - rows)], small_send.at[kind])
        arrived(hid.at[pl.ds(0, pairs)], hid_send)
        arrived(out0, fold_send.at[0])
        arrived(out1, fold_send.at[1])
        arrived(last_in, last_send)


def fused_plan(mesh, rows, width, local_count, units):
    n_ep, n_dp, n_tp = (mesh.shape[a] for a in ("ep", "dp", "tp"))
    if n_dp != 2 or local_count % 4 or n_ep != 4 or rows % 8 or rows % n_tp:
        return None
    if units % 128 or width % 1024:
        return None
    pairs = local_count // 4
    chunks = width // 1024
    total_rows = 2 * n_ep * rows
    hidden = local_count * units
    slot = 1024 * 4 * units * 2
    pad = -(-(rows // n_tp) // 8) * 8
    held = total_rows * width * 2 + hidden * width + pairs * total_rows * 4 * units * 4
    held += total_rows * hidden * 2 + (total_rows // 2) * (width // 2) * 12
    held += pad * width * (n_tp * 6 + 8 * n_tp) + 5_000_000
    ring = min(chunks * pairs, (VMEM_BYTES - held) // slot)
    if ring < 2 * pairs or pairs < 2 or 4 * units < 512:
        return None
    return chunks, pairs, ring


def fused(mesh, plan, tokens, expert_ids, route_weight, gate_weight, up_weight, down_weight):
    chunks, pairs, ring = plan
    n_ep, n_tp = mesh.shape["ep"], mesh.shape["tp"]
    rows, width = tokens.shape
    units = gate_weight.shape[2]
    wide = 512
    blocks = width // 2 // wide
    depth = width // chunks
    total_rows = 2 * n_ep * rows
    out_rows = rows // n_tp
    top = expert_ids.shape[1]
    sub = wide // 2
    dma = pltpu.SemaphoreType.DMA
    f32, bf16 = jnp.float32, jnp.bfloat16
    return pl.pallas_call(
        partial(moe_kernel, n_ep, n_tp, ring, min(EARLY, ring)),
        out_shape=jax.ShapeDtypeStruct((out_rows, width), bf16),
        in_specs=[pl.BlockSpec(memory_space=pltpu.HBM)] * 6,
        out_specs=pl.BlockSpec(memory_space=pltpu.VMEM),
        scratch_shapes=[
            pltpu.VMEM((chunks, 2, 2 * n_ep, rows, depth // 2), bf16),
            pltpu.VMEM((top, rows), jnp.int32),
            pltpu.VMEM((top, rows), f32),
            pltpu.VMEM((total_rows, top), jnp.int32),
            pltpu.VMEM((total_rows, top), f32),
            pltpu.VMEM((ring, depth, 4 * units), bf16),
            pltpu.VMEM((blocks, 4 * pairs, units, wide), bf16),
            pltpu.VMEM((pairs, total_rows, 4 * units), f32),
            pltpu.VMEM((2 * pairs, total_rows, 2 * units), bf16),
            pltpu.VMEM((blocks, 2, 2, n_ep // 2, rows, sub), f32),
            pltpu.VMEM((blocks, 2, 2, n_ep // 2, rows, sub), bf16),
            pltpu.VMEM((blocks, 2, 2, n_ep // 2, rows, sub), bf16),
            pltpu.VMEM((blocks, 2, 2, rows, sub), bf16),
            pltpu.VMEM((blocks, 2, 2, rows, sub), bf16),
            pltpu.VMEM((blocks, n_tp, out_rows, wide), f32),
            pltpu.VMEM((blocks, 2, n_tp, out_rows, wide), bf16),
            pltpu.VMEM((blocks, 2 * n_tp - 1, out_rows, wide), bf16),
            dma((3,)),
            dma((2,)),
            dma((2,)),
            dma,
            dma((chunks, 3)),
            dma((ring,)),
            dma((blocks,)),
            dma,
            dma((pairs,)),
            dma((2,)),
            dma((blocks, 2)),
            dma,
            dma((blocks,)),
        ],
        compiler_params=pltpu.CompilerParams(
            collective_id=0, has_side_effects=True, vmem_limit_bytes=VMEM_BYTES
        ),
    )(tokens, expert_ids.T, route_weight.T, gate_weight, up_weight, down_weight)


def solution(mesh):
    in_specs = (
        P(("ep", "dp"), None),
        P(("ep", "dp"), None),
        P(("ep", "dp"), None),
        P("ep", None, "tp"),
        P("ep", None, "tp"),
        P("ep", "tp", None),
    )
    out_specs = P(("ep", "dp", "tp"), None)

    def body(*arrays):
        rows, width = arrays[0].shape
        local_count, _, units = arrays[3].shape
        plan = fused_plan(mesh, rows, width, local_count, units)
        if plan is None:
            return per_device(*arrays)
        return fused(mesh, plan, *arrays)

    return jax.shard_map(body, mesh=mesh, in_specs=in_specs, out_specs=out_specs, check_vma=False)
```

time: 72.9 us -> 48.6 us (0.67)
  Pallas kernels: 68.4 us -> 46.8 us
  local copies, waits for them, and re-layouts: 4.27 us -> 1.55 us
    pallas_call x1, Pallas kernels: 68.4 us -> 46.8 us  [fused(): pl.pallas_call(partial(moe_kernel, n_ep, n_tp, ring, min(EARLY, ring)), o...]
    unnamed x3 -> x1, local copies, waits for them, and re-layouts: 4.27 us -> 1.55 us
where the time goes in v1:
time: 48.6 us; the launch traced here: 48.4 us
  Pallas kernels  46.8 us (96%)
  local copies, waits for them, and re-layouts  1.55 us (3%)
    pallas_call x1, Pallas kernels, fused(): pl.pallas_call(partial(moe_kernel, n_ep, n_tp, ring, min(EARLY, ring)), o...  46.8 us
    unnamed x1, local copies, waits for them, and re-layouts  1.55 us

profile of v1, /device:TPU:0, one launch (start us, length us, event | category | flops | bytes accessed | tf_op | source)
XLA Modules:
  0.0 48.4 jit_solution(16775184017608918626)
XLA Ops:
  0.0 46.8 %shard_map.64 = bf16[6,7168]{1,0:T(8,128)(2,1)} custom-call(bf16[24,7168]{1,0:T(8,128)(2,1)} %tok_ref.1, s32[8,24]{1,0:T(8,128)} %bitcast.2, f32[8,24]{1,0:T(8,128)} %bitcast.3, bf16[8,7168,384]{2,1,0:T(8,128)(2,1)} %gate_ref.1, bf16[8,7168,384]{2,1,0:T(8,128)(2,1)} %up_ref.1, bf16[8,384,7168]{2,1,0:T(8,128)(2,1)} %down_ref.1), custom_call_target="tpu_custom_call" | custom-call | tf_op jit(solution)/shard_map/pallas_call | solution.py:465
  46.8 1.6 %copy.8 = bf16[6,7168]{1,0:T(8,128)(2,1)} copy(bf16[6,7168]{1,0:T(8,128)(2,1)} %shard_map.64) | data formatting | bytes 172032

commit v2 on v1

--- a/solution.py
+++ b/solution.py
@@ -15,6 +15,7 @@
 AHEAD = 4
 EARLY = 5
 LAGS = (3, 5, 9)
+Z_TURNS = (7, 9, 11)
 
 
 def expert_block(received, gate_weight, up_weight, down_weight):
@@ -96,8 +97,10 @@
     out_ref,
     xs, ids_own, rw_own, ids_all, rw_all, gu, dn, acc, hid, own, out0, in0, out1, in1,
     last_keep, last_out, last_in,
+    zkeep, zout, zin, zown, zout0, zin0, zout1, zin1, zlast_keep, zlast_out, zlast_in,
     in_sem, small_send, small_recv, ag_send, ag_recv, gu_sem, dn_sem, hid_send, hid_recv,
-    fold_send, fold_recv, last_send, last_recv,
+    fold_send, fold_recv, last_send, last_recv, out_v, out_sem,
+    zsend, zrecv, zfold_send, zfold_recv, zlast_send, zlast_recv,
 ):
     ep, dp, tp = lax.axis_index("ep"), lax.axis_index("dp"), lax.axis_index("tp")
     rows = tok_ref.shape[0]
@@ -119,6 +122,7 @@
     other_first = (1 - dp) * experts
     sibling = {"dp": 1 - dp}
     column = dp * half
+    z_block = 1
 
     def arrived(ref, sem):
         pltpu.make_async_copy(ref, ref, sem).wait()
@@ -214,14 +218,16 @@
     lead = min(AHEAD, chunks)
     for chunk in range(lead):
         gather(chunk, 0)
-    for q, other in group:
-        device = {"ep": xor_any(ep, q), "dp": 1 - dp if other else dp}
-        row = (other * n_ep + q) * rows
-        for kind, ref in enumerate((ids_all, rw_all)):
-            send(
-                ref.at[pl.ds(0, rows), :], ref.at[pl.ds(row, rows), :],
-                small_send.at[kind], small_recv.at[kind], device,
-            )
+    def share_routes():
+        for q, other in group:
+            device = {"ep": xor_any(ep, q), "dp": 1 - dp if other else dp}
+            row = (other * n_ep + q) * rows
+            for kind, ref in enumerate((ids_all, rw_all)):
+                send(
+                    ref.at[pl.ds(0, rows), :], ref.at[pl.ds(row, rows), :],
+                    small_send.at[kind], small_recv.at[kind], device,
+                )
+
     asked = 0
 
     def relay():
@@ -232,6 +238,8 @@
             if asked + lead < chunks:
                 gather(asked + lead, 0)
             asked += 1
+            if asked == chunks:
+                share_routes()
 
     for _ in range(lead):
         relay()
@@ -381,6 +389,77 @@
                         last_send, last_recv.at[n], {"dp": to, "tp": peer},
                     )
 
+    def put(start, value):
+        cols = pl.ds(pl.multiple_of(start, 128), wide)
+        out_v[:, cols] = value.astype(out_ref.dtype)
+        pltpu.make_async_copy(out_v.at[:, cols], out_ref.at[:, cols], out_sem).start()
+
+    def z_store(value):
+        for t in range(n_tp):
+            for g in range(groups):
+                row = g * rows + t * out_rows
+                piece = value[row : row + out_rows]
+                zkeep[t, g] = piece
+                zout[t, g] = piece.astype(jnp.bfloat16)
+        for step in range(1, n_tp):
+            peer = lax.rem(tp + step, n_tp)
+            send(zout.at[peer], zin.at[step - 1], zsend, zrecv, {"tp": peer})
+
+    def z_fold(src, dst, step):
+        for side in range(2):
+            bit, _, _ = split(side, step)
+            send(
+                src.at[side], dst.at[side], zfold_send.at[step], zfold_recv.at[step],
+                {"ep": xor_bit(ep, bit)},
+            )
+
+    def z_fold0():
+        arrived(zin, zrecv)
+        for d in range(2):
+            for q in range(n_ep):
+                total = zkeep[tp, d * n_ep + q]
+                for t in range(n_tp - 1):
+                    total += zin[t, d * n_ep + q].astype(jnp.float32)
+                for side in range(2):
+                    _, kept, away = split(side, 0)
+                    part = total[:, side * sub : (side + 1) * sub]
+                    if q in away:
+                        zout0[side, d, away.index(q)] = part.astype(jnp.bfloat16)
+                    else:
+                        zown[side, d, kept.index(q)] = part
+        z_fold(zout0, zin0, 0)
+
+    def z_fold1():
+        arrived(zin0, zfold_recv.at[0])
+        for side in range(2):
+            _, held, _ = split(side, 0)
+            _, kept, away = split(side, 1)
+            at_away, at_kept = held.index(away[0]), held.index(kept[0])
+            for d in range(2):
+                total = zown[side, d, at_away] + zin0[side, d, at_away].astype(jnp.float32)
+                zout1[side, d] = total.astype(jnp.bfloat16)
+                zown[side, d, at_kept] += zin0[side, d, at_kept].astype(jnp.float32)
+        z_fold(zout1, zin1, 1)
+
+    def z_fold2():
+        arrived(zin1, zfold_recv.at[1])
+        for side in range(2):
+            _, held, _ = split(side, 0)
+            at_kept = held.index(0)
+            cols = slice(side * sub, (side + 1) * sub)
+            for d in range(2):
+                total = zown[side, d, at_kept] + zin1[side, d].astype(jnp.float32)
+                if d:
+                    zlast_out[:, cols] = total.astype(jnp.bfloat16)
+                else:
+                    zlast_keep[:, cols] = total
+        send(zlast_out, zlast_in, zlast_send, zlast_recv, sibling)
+
+    def z_finish():
+        arrived(zlast_in, zlast_recv)
+        put(dp * half + z_block * wide, zlast_keep[...])
+        put((1 - dp) * half + z_block * wide, zlast_in[...])
+
     def finish(n):
         arrived(last_in.at[n], last_recv.at[n])
         for other in range(2):
@@ -389,10 +468,10 @@
                 if step or other:
                     value += last_in[n, step * 2 + other - 1].astype(jnp.float32)
             start = (1 - dp if other else dp) * half + n * wide
-            out_ref[:, pl.ds(pl.multiple_of(start, 128), wide)] = value.astype(out_ref.dtype)
+            put(start, value)
 
     def stage(n, fn, name):
-        if 0 <= n < blocks:
+        if 0 <= n < blocks and n != z_block:
             with jax.named_scope(f"{name}#n={n}"):
                 fn(n)
 
@@ -412,19 +491,33 @@
                 else:
                     arrived(dn.at[turn], dn_sem.at[turn])
                     value = down(turn, 0, 2 * pairs)
-                store0(turn, value)
+                if turn == z_block:
+                    z_store(value)
+                else:
+                    store0(turn, value)
         stage(turn - LAGS[0], fold1, "fold1")
         stage(turn, fold0, "fold0")
         stage(turn - LAGS[1], fold2, "fold2")
         stage(turn - LAGS[2], finish, "finish")
+        for at, fn in zip(Z_TURNS, (z_fold0, z_fold1, z_fold2)):
+            if turn == at:
+                with jax.named_scope(f"z#n={at}"):
+                    fn()
+    with jax.named_scope("zfin"):
+        z_finish()
     with jax.named_scope("tailsend"):
         arrived(xs.at[:, :, pl.ds(0, groups - 1)], ag_send)
         for kind, ref in enumerate((ids_all, rw_all)):
             arrived(ref.at[pl.ds(rows, total_rows - rows)], small_send.at[kind])
         arrived(hid.at[pl.ds(0, pairs)], hid_send)
-        arrived(out0, fold_send.at[0])
-        arrived(out1, fold_send.at[1])
-        arrived(last_in, last_send)
+        arrived(out0.at[pl.ds(0, blocks - 1)], fold_send.at[0])
+        arrived(out1.at[pl.ds(0, blocks - 1)], fold_send.at[1])
+        arrived(last_in.at[pl.ds(0, blocks - 1)], last_send)
+        arrived(zin, zsend)
+        arrived(zout0, zfold_send.at[0])
+        arrived(zout1, zfold_send.at[1])
+        arrived(zlast_out, zlast_send)
+        pltpu.make_async_copy(out_v, out_ref, out_sem).wait()
 
 
 def fused_plan(mesh, rows, width, local_count, units):
@@ -441,9 +534,9 @@
     pad = -(-(rows // n_tp) // 8) * 8
     held = total_rows * width * 2 + hidden * width + pairs * total_rows * 4 * units * 4
     held += total_rows * hidden * 2 + (total_rows // 2) * (width // 2) * 12
-    held += pad * width * (n_tp * 6 + 8 * n_tp) + 5_000_000
+    held += pad * width * (n_tp * 6 + 8 * n_tp) + 5_800_000
     ring = min(chunks * pairs, (VMEM_BYTES - held) // slot)
-    if ring < 2 * pairs or pairs < 2 or 4 * units < 512:
+    if ring < 2 * pairs or pairs < 2 or chunks < 2 or 4 * units < 512:
         return None
     return chunks, pairs, ring
 
@@ -466,7 +559,7 @@
         partial(moe_kernel, n_ep, n_tp, ring, min(EARLY, ring)),
         out_shape=jax.ShapeDtypeStruct((out_rows, width), bf16),
         in_specs=[pl.BlockSpec(memory_space=pltpu.HBM)] * 6,
-        out_specs=pl.BlockSpec(memory_space=pltpu.VMEM),
+        out_specs=pl.BlockSpec(memory_space=pltpu.HBM),
         scratch_shapes=[
             pltpu.VMEM((chunks, 2, 2 * n_ep, rows, depth // 2), bf16),
             pltpu.VMEM((top, rows), jnp.int32),
@@ -485,6 +578,17 @@
             pltpu.VMEM((blocks, n_tp, out_rows, wide), f32),
             pltpu.VMEM((blocks, 2, n_tp, out_rows, wide), bf16),
             pltpu.VMEM((blocks, 2 * n_tp - 1, out_rows, wide), bf16),
+            pltpu.VMEM((n_tp, 2 * n_ep, out_rows, wide), f32),
+            pltpu.VMEM((n_tp, 2 * n_ep, out_rows, wide), bf16),
+            pltpu.VMEM((n_tp - 1, 2 * n_ep, out_rows, wide), bf16),
+            pltpu.VMEM((2, 2, n_ep // 2, out_rows, sub), f32),
+            pltpu.VMEM((2, 2, n_ep // 2, out_rows, sub), bf16),
+            pltpu.VMEM((2, 2, n_ep // 2, out_rows, sub), bf16),
+            pltpu.VMEM((2, 2, out_rows, sub), bf16),
+            pltpu.VMEM((2, 2, out_rows, sub), bf16),
+            pltpu.VMEM((out_rows, wide), f32),
+            pltpu.VMEM((out_rows, wide), bf16),
+            pltpu.VMEM((out_rows, wide), bf16),
             dma((3,)),
             dma((2,)),
             dma((2,)),
@@ -498,6 +602,14 @@
             dma((blocks, 2)),
             dma,
             dma((blocks,)),
+            pltpu.VMEM((out_rows, width), bf16),
+            dma,
+            dma,
+            dma,
+            dma((2,)),
+            dma((2,)),
+            dma,
+            dma,
         ],
         compiler_params=pltpu.CompilerParams(
             collective_id=0, has_side_effects=True, vmem_limit_bytes=VMEM_BYTES

time: 48.6 us -> 46.4 us (0.955)
  Pallas kernels: 46.8 us -> 44.7 us
    pallas_call x1, Pallas kernels: 46.8 us -> 44.7 us  [fused(): pl.pallas_call(partial(moe_kernel, n_ep, n_tp, ring, min(EARLY, ring)), o...]
where the time goes in v2:
time: 46.4 us; the launch traced here: 46.2 us
  Pallas kernels  44.7 us (96%)
  local copies, waits for them, and re-layouts  1.55 us (3%)
    pallas_call x1, Pallas kernels, fused(): pl.pallas_call(partial(moe_kernel, n_ep, n_tp, ring, min(EARLY, ring)), o...  44.7 us
    unnamed x1, local copies, waits for them, and re-layouts  1.55 us

profile of v2, /device:TPU:0, one launch (start us, length us, event | category | flops | bytes accessed | tf_op | source)
XLA Modules:
  0.0 46.2 jit_solution(14334913908049741581)
XLA Ops:
  0.0 44.7 %shard_map.64 = bf16[6,7168]{1,0:T(8,128)(2,1)} custom-call(bf16[24,7168]{1,0:T(8,128)(2,1)} %tok_ref.1, s32[8,24]{1,0:T(8,128)} %bitcast.2, f32[8,24]{1,0:T(8,128)} %bitcast.3, bf16[8,7168,384]{2,1,0:T(8,128)(2,1)} %gate_ref.1, bf16[8,7168,384]{2,1,0:T(8,128)(2,1)} %up_ref.1, bf16[8,384,7168]{2,1,0:T(8,128)(2,1)} %down_ref.1), custom_call_target="tpu_custom_call" | custom-call | tf_op jit(solution)/shard_map/pallas_call | solution.py:558
  44.7 1.6 %copy.8 = bf16[6,7168]{1,0:T(8,128)(2,1)} copy(bf16[6,7168]{1,0:T(8,128)(2,1)} %shard_map.64) | data formatting | bytes 172032
